TPU v7x, 32 devices: a whole 2x2x4 slice. The times are simulated.
32 devices in a mesh: expert: 8 (over y, x, core), dp: 4 (over z).
Axes of the slice: x: 2, y: 2, z: 4, core: 2. Of those that a mesh axis runs over, the one named last changes fastest.
Arguments:
- patches: bfloat16 [8192, 1024], P(('expert', 'dp')), may hold values from -6 to 6
- router_weight: bfloat16 [1024, 8], replicated, may hold values from -0.1875 to 0.1875
- router_bias: float32 [8], replicated, may hold values from -1.5 to 1.5
- noise: float32 [8192, 8], P(('expert', 'dp')), may hold values from -5 to 5
- top_experts: int32 [8192, 2], P(('expert', 'dp')), may hold values from 0 to 7, all different within a row; in each aligned block of 256 rows (0 to 255, 256 to 511, ...) at most 80 rows name the same one
- threshold_expert: int32 [8192], P(('expert', 'dp')), may hold values from 0 to 7
- w_in: bfloat16 [8, 1024, 2048], P('expert'), may hold values from -0.1875 to 0.1875
- w_out: bfloat16 [8, 2048, 1024], P('expert'), may hold values from -0.125 to 0.125
- out_grad: bfloat16 [8192, 1024], P(('expert', 'dp')), may hold values from -24 to 24
Outputs:
- patch_grad: bfloat16 [8192, 1024], P(('expert', 'dp'))
- w_in_grad: bfloat16 [8, 1024, 2048], P('expert', None, 'dp')
- w_out_grad: bfloat16 [8, 2048, 1024], P('expert', 'dp')
- router_weight_grad: float32 [1024, 8], replicated
- router_bias_grad: float32 [8], replicated
Inputs may be any that keep to these rules, and one draw needn't show every extreme that they name: `top_experts`: the two experts of a patch differ; among the patches of one device no expert is named more than 80 times.
All inputs are finite; a program needn't handle non-finite values.
Results may differ from a plain program's by a relative error of at most 0.0062.
The roundings to bfloat16 on the way count: a program that leaves them out, or rounds other values in their place, can miss the bound.
Values may be sent and summed in bfloat16 or wider, within the bound.
A program may use at most 128 MiB of HBM per device.

v0:
```python
import jax
import jax.numpy as jnp
from jax import lax
from jax.sharding import PartitionSpec as P

noise_std = 1.0
aux_weight = 1.0
inv_root_two = 0.7071067811865476
inv_root_tau = 0.3989422804014327


def gelu_tanh(values):
    return jax.nn.gelu(values, approximate=True)


def spread_grad(values):
    number = values.shape[0]
    average = jnp.mean(values)
    spread = jnp.mean((values - average) ** 2)
    return (2.0 * (values - average) - 2.0 * spread / average) / (number * average * average)


def expert_local(rows_in, rows_grad, rows_gate, w_first, w_second):
    hidden = jnp.dot(rows_in, w_first, preferred_element_type=jnp.float32)
    active, pullback = jax.vjp(gelu_tanh, hidden)
    active_low = lax.optimization_barrier(active.astype(jnp.bfloat16))
    back_proj = jnp.dot(rows_grad, w_second.T, preferred_element_type=jnp.float32)
    gate_col = rows_gate.astype(jnp.float32)[:, None]
    gate_terms = jnp.sum(back_proj * active_low.astype(jnp.float32), axis=-1)
    hidden_grad = pullback(gate_col * back_proj)[0].astype(jnp.bfloat16)
    scaled_grad = (gate_col * rows_grad.astype(jnp.float32)).astype(jnp.bfloat16)
    first_grad = jnp.dot(rows_in.T, hidden_grad, preferred_element_type=jnp.float32)
    second_grad = jnp.dot(active_low.T, scaled_grad, preferred_element_type=jnp.float32)
    return (first_grad, second_grad, hidden_grad, gate_terms)


def expert_terms(rows_in, rows_grad, rows_gate, w_first, w_second):
    first_grad, second_grad, hidden_grad, gate_terms = expert_local(
        rows_in, rows_grad, rows_gate, w_first, w_second
    )
    rows_back = jnp.dot(hidden_grad, w_first.T, preferred_element_type=jnp.float32)
    return (first_grad, second_grad, rows_back, gate_terms)


def on_device(
    patches, router_weight, router_bias, noise, top_experts, threshold_expert, w_in, w_out, out_grad
):
    tok_rows = patches.shape[0]
    width = patches.shape[1]
    experts = router_weight.shape[1]
    capacity = 5 * tok_rows // (2 * experts)
    slots = experts * capacity
    total_tokens = tok_rows * lax.axis_size("expert") * lax.axis_size("dp")
    logits = jnp.dot(patches, router_weight, preferred_element_type=jnp.float32) + router_bias
    noisy = logits + noise_std * noise
    probs = jax.nn.softmax(noisy, axis=-1)
    expert_ids = lax.broadcasted_iota(jnp.int32, (1, experts), 1)
    thresh_hot = threshold_expert[:, None] == expert_ids
    base = jnp.sum(jnp.where(thresh_hot, noisy, 0.0), axis=-1, keepdims=True)
    zscore = (logits - base) / noise_std
    importance, load = lax.psum(
        (jnp.sum(probs, axis=0), jnp.sum(0.5 * (1.0 + lax.erf(zscore * inv_root_two)), axis=0)),
        ("expert", "dp"),
    )
    top_hot = top_experts[:, :, None] == expert_ids[None]
    gates = jnp.sum(jnp.where(top_hot, probs[:, None, :], 0.0), axis=-1).astype(jnp.bfloat16)
    flat = top_experts.reshape(-1)
    flat_hot = (flat[:, None] == expert_ids).astype(jnp.int32)
    before = jnp.sum((jnp.cumsum(flat_hot, axis=0) - flat_hot) * flat_hot, axis=-1)
    slot_ids = flat * capacity + before
    slot_index = lax.broadcasted_iota(jnp.int32, (slots, 1), 0)
    assign = (slot_index == slot_ids[None, :]).astype(jnp.bfloat16)
    assign_tok = jnp.sum(assign.reshape(slots, tok_rows, 2), axis=-1)
    sent_in = (
        jnp.dot(assign_tok, patches, preferred_element_type=jnp.float32)
        .astype(jnp.bfloat16)
        .reshape(experts, capacity, width)
    )
    sent_grad = (
        jnp.dot(assign_tok, out_grad, preferred_element_type=jnp.float32)
        .astype(jnp.bfloat16)
        .reshape(experts, capacity, width)
    )
    sent_gate = (
        jnp.dot(assign, gates.reshape(-1), preferred_element_type=jnp.float32)
        .astype(jnp.bfloat16)
        .reshape(experts, capacity)
    )
    recv_in, recv_grad, recv_gate = (
        lax.all_to_all(sent_in, "expert", split_axis=0, concat_axis=0, tiled=True),
        lax.all_to_all(sent_grad, "expert", split_axis=0, concat_axis=0, tiled=True),
        lax.all_to_all(sent_gate, "expert", split_axis=0, concat_axis=0, tiled=True),
    )
    rows_in = recv_in.reshape(slots, width)
    rows_grad = recv_grad.reshape(slots, width)
    rows_gate = recv_gate.reshape(slots)
    w_first = w_in[0]
    w_second = w_out[0]
    first_grad, second_grad, rows_back, gate_terms = expert_terms(
        rows_in, rows_grad, rows_gate, w_first, w_second
    )
    first_part, second_part = (
        lax.psum_scatter(first_grad, "dp", scatter_dimension=1, tiled=True),
        lax.psum_scatter(second_grad, "dp", scatter_dimension=0, tiled=True),
    )
    back_rows = rows_back.astype(jnp.bfloat16).reshape(experts, capacity, width)
    back_gate = gate_terms.astype(jnp.bfloat16).reshape(experts, capacity)
    home_rows, home_gate = (
        lax.all_to_all(back_rows, "expert", split_axis=0, concat_axis=0, tiled=True),
        lax.all_to_all(back_gate, "expert", split_axis=0, concat_axis=0, tiled=True),
    )
    expert_back = jnp.dot(
        assign_tok.T, home_rows.reshape(slots, width), preferred_element_type=jnp.float32
    )
    gate_grad = jnp.dot(
        home_gate.reshape(slots), assign, preferred_element_type=jnp.float32
    ).reshape(tok_rows, 2)
    total_weight = aux_weight * total_tokens
    imp_coef = total_weight * spread_grad(importance)
    load_coef = total_weight * spread_grad(load)
    score_grad = jnp.sum(jnp.where(top_hot, gate_grad[:, :, None], 0.0), axis=1) + imp_coef[None, :]
    noisy_grad = probs * (score_grad - jnp.sum(probs * score_grad, axis=-1, keepdims=True))
    z_grad = load_coef[None, :] * inv_root_tau * jnp.exp(-0.5 * zscore * zscore)
    logit_grad = (
        noisy_grad
        + z_grad / noise_std
        - jnp.where(thresh_hot, jnp.sum(z_grad, axis=-1, keepdims=True) / noise_std, 0.0)
    )
    logit_low = logit_grad.astype(jnp.bfloat16)
    router_back = jnp.dot(logit_low, router_weight.T, preferred_element_type=jnp.float32)
    patch_grad = (expert_back + router_back).astype(jnp.bfloat16)
    weight_part = jnp.dot(patches.T, logit_low, preferred_element_type=jnp.float32)
    router_weight_grad, router_bias_grad = lax.psum(
        (weight_part, jnp.sum(logit_grad, axis=0)), ("expert", "dp")
    )
    return (
        patch_grad,
        first_part.astype(jnp.bfloat16)[None],
        second_part.astype(jnp.bfloat16)[None],
        router_weight_grad,
        router_bias_grad,
    )


def solution(mesh):
    placed = (
        P(("expert", "dp"), None),
        P(),
        P(),
        P(("expert", "dp"), None),
        P(("expert", "dp"), None),
        P(("expert", "dp")),
        P("expert", None, None),
        P("expert", None, None),
        P(("expert", "dp"), None),
    )
    return jax.shard_map(
        on_device,
        mesh=mesh,
        in_specs=placed,
        out_specs=(
            P(("expert", "dp"), None),
            P("expert", None, "dp"),
            P("expert", "dp", None),
            P(),
            P(),
        ),
        check_vma=False,
    )
```

profile of v0, /device:TPU:0, one launch (start us, length us, event | category | flops | bytes accessed | tf_op | source)
XLA Modules:
  0.0 399.7 jit_solution(11020807704980809299)
XLA Ops:
  7.2 0.9 copy.39
  8.1 0.1 eq.91
  8.3 0.1 eq.87
  8.4 1.1 reduce-window.6
  9.6 0.2 slice_reduce_fusion
  9.8 0.1 fusion.26
  9.9 0.1 reduce_sum.150
  10.1 0.7 multiply_add_fusion.1
  10.8 0.3 fusion.23
  11.1 1.6 convolution_convert_fusion
  12.7 5.3 %all-to-all-start.2 = ((bf16[8,80,1024]{2,1,0:T(8,128)(2,1)}), bf16[8,80,1024]{2,1,0:T(8,128)(2,1)S(1)}, u32[]{:S(2)}, u32[]{:S(2)}) async-start(bf16[8,80,1024]{2,1,0:T(8,128)(2,1)} %bitcast.6), calls=%async_computation.2 | async-start | bytes 2621440 | tf_op jit(solution)/shard_map/all_to_all | solution.py:90
  18.1 0.3 fusion.38
  18.3 1.6 convolution_convert_fusion.1
  19.9 16.3 %all-to-all-done.2 = bf16[8,80,1024]{2,1,0:T(8,128)(2,1)S(1)} async-done(((bf16[8,80,1024]{2,1,0:T(8,128)(2,1)}), bf16[8,80,1024]{2,1,0:T(8,128)(2,1)S(1)}, u32[]{:S(2)}, u32[]{:S(2)}) %all-to-all-start.2) | async-done | bytes 1310752 | tf_op jit(solution)/shard_map/all_to_all | solution.py:90
  36.2 3.6 all-to-all-start.1
  39.8 1.0 iota_compare_fusion
  40.8 8.1 %multiply_convert_fusion = (bf16[640,2048]{1,0:T(8,128)(2,1)}, f32[640,2048]{1,0:T(8,128)}) fusion(bf16[640,1024]{1,0:T(8,128)(2,1)S(1)} %bitcast.58, bf16[1,1024,2048]{2,1,0:T(8,128)(2,1)} %param.15), kind=kOutput, calls=%fused_computation.10 | convolution fusion | flops 2696151040 | bytes 13369344 | tf_op jit(solution)/shard_map/dot_general | solution.py:24
  48.9 9.0 %all-to-all-done.1 = bf16[8,80,1024]{2,1,0:T(8,128)(2,1)S(1)} async-done(((bf16[8,80,1024]{2,1,0:T(8,128)(2,1)}), bf16[8,80,1024]{2,1,0:T(8,128)(2,1)S(1)}, u32[]{:S(2)}, u32[]{:S(2)}) %all-to-all-start.1) | async-done | bytes 1310752 | tf_op jit(solution)/shard_map/all_to_all | solution.py:91
  57.9 8.8 %multiply_reduce_fusion = (bf16[640]{0:T(1024)(128)(2,1)S(1)}, f32[640,2048]{1,0:T(8,128)}) fusion(bf16[640,2048]{1,0:T(8,128)(2,1)} %get-tuple-element.19, bf16[640,1024]{1,0:T(8,128)(2,1)S(1)} %bitcast.60, bf16[1,2048,1024]{2,1,0:T(8,128)(2,1)} %param.16), kind=kOutput, calls=%fused_computation.9 | convolution fusion | flops 2688286208 | bytes 13370624 | tf_op jit(solution)/shard_map/dot_general | solution.py:27
  66.7 0.7 convert_element_type.106
  67.4 3.3 all-to-all-start.4
  70.7 0.2 fusion.36
  70.9 0.4 eq.106
  71.3 3.9 all-to-all-done.4
  75.3 0.9 fusion.16
  76.4 0.1 copy.42
  76.5 0.2 reshape.149
  76.7 0.3 fusion.22
  77.1 7.1 %all_to_all.31 = bf16[8,1,80]{2,1,0:T(2,128)(2,1)S(1)} all-to-all(bf16[8,1,80]{2,1,0:T(2,128)(2,1)S(1)} %all_to_all.25), channel_id=1, replica_groups=mesh['expert'=8,'dp'=4] {'expert'}, dimensions={0} | all-to-all | bytes 2560 | tf_op jit(solution)/shard_map/all_to_all | solution.py:92
  84.3 6.5 %fusion.6 = bf16[640,2048]{1,0:T(8,128)(2,1)S(1)} fusion(f32[640,2048]{1,0:T(8,128)} %get-tuple-element.20, f32[640,2048]{1,0:T(8,128)} %get-tuple-element.22, f32[640]{0:T(1024)S(1)} %reshape.148), kind=kLoop, calls=%fused_computation.8 | loop fusion | flops 27525120 | bytes 13109760 | tf_op jit(solution)/shard_map/convert_element_type | solution.py:30
  90.8 5.7 %fusion.40 = f32[1024,2048]{1,0:T(8,128)} fusion(bf16[640,1024]{1,0:T(8,128)(2,1)S(1)} %bitcast.59, bf16[640,2048]{1,0:T(8,128)(2,1)S(1)} %fusion.6), kind=kOutput, calls=%fused_computation.74 | convolution fusion | flops 2684354560 | bytes 12320768 | tf_op jit(solution)/shard_map/dot_general | solution.py:32
  96.5 8.9 %fusion.17 = f32[2048,1024]{1,0:T(8,128)} fusion(bf16[640,2048]{1,0:T(8,128)(2,1)} %get-tuple-element.19, bf16[640,1024]{1,0:T(8,128)(2,1)} %bitcast.61, f32[640]{0:T(1024)S(1)} %reshape.148), kind=kOutput, calls=%fused_computation.24 | convolution fusion | flops 2686320640 | bytes 12323328 | tf_op jit(solution)/shard_map/dot_general | solution.py:33
  105.4 43.9 %all-reduce.1 = (f32[8]{0:T(128)S(1)}, f32[8]{0:T(128)S(1)}) all-reduce(f32[8]{0:T(128)S(1)} %get-tuple-element.24, f32[8]{0:T(128)S(1)} %get-tuple-element.15), channel_id=1, replica_groups=mesh['expert'=8,'dp'=4] {'expert','dp'}, use_global_device_ids=true, to_apply=%region_16.17 | all-reduce | flops 16 | bytes 128 | tf_op jit(solution)/shard_map/psum | solution.py:61
  149.3 0.6 reduce_sum.162
  151.2 0.6 multiply_reduce_fusion.3
  152.5 0.6 reduce_sum.157
  154.4 0.6 multiply_reduce_fusion.4
  155.7 6.4 %fusion.13 = bf16[640,1024]{1,0:T(8,128)(2,1)} fusion(bf16[640,2048]{1,0:T(8,128)(2,1)S(1)} %fusion.6, bf16[1,1024,2048]{2,1,0:T(8,128)(2,1)} %param.15), kind=kOutput, calls=%fused_computation.19 | convolution fusion | flops 2685009920 | bytes 8126464 | tf_op jit(solution)/shard_map/dot_general | solution.py:41
  162.1 3.9 all-to-all-start.3
  166.1 0.2 fusion.35
  166.3 0.2 convolution_bitcast_fusion
  166.5 52.9 %all-reduce = (f32[1024,8]{0,1:T(8,128)}, f32[8]{0:T(128)}) all-reduce(f32[1024,8]{0,1:T(8,128)S(1)} %convolution_bitcast_fusion, f32[8]{0:T(128)S(1)} %get-tuple-element.13), channel_id=1, replica_groups=mesh['expert'=8,'dp'=4] {'expert','dp'}, use_global_device_ids=true, to_apply=%region_22.23 | all-reduce | flops 8200 | bytes 65600 | tf_op jit(solution)/shard_map/psum | solution.py:133
  219.4 0.6 fusion.39
  220.0 1.1 fusion.21
  221.1 21.5 %reduce-scatter.3.cloned.1.call-done = f32[1024,512]{1,0:T(8,128)} async-done(((f32[1024,2048]{1,0:T(8,128)}), f32[1024,512]{1,0:T(8,128)}) %reduce-scatter.3.cloned.1.call-update) | async-done | bytes 2097168 | tf_op jit(solution)/shard_map/reduce_scatter | solution.py:103
  242.6 2.7 convert_bitcast_fusion.1
  245.3 144.8 %reduce-scatter.5.cloned.1.call-done = f32[512,1024]{1,0:T(8,128)} async-done(((f32[2048,1024]{1,0:T(8,128)}), f32[512,1024]{1,0:T(8,128)}) %reduce-scatter.5.cloned.1.call-update) | async-done | bytes 2097168 | tf_op jit(solution)/shard_map/reduce_scatter | solution.py:104
  390.1 2.7 convert_bitcast_fusion
  (45 shorter events, 0.9 us)
Async XLA Ops:
  7.2 3.9 copy-start
  7.2 10.8 %copy-start.8 = (f32[256,8]{0,1:T(8,128)S(1)}, f32[256,8]{0,1:T(8,128)}, u32[]{:S(2)}) copy-start(f32[256,8]{0,1:T(8,128)} %param.12) | copy-start | bytes 24580
  7.2 10.8 %copy-start.10 = (f32[8]{0:T(128)S(1)}, f32[8]{0:T(128)}, u32[]{:S(2)}) copy-start(f32[8]{0:T(128)} %param.11) | copy-start | bytes 100
  7.2 10.8 %copy-start.6 = (bf16[1024,8]{0,1:T(8,128)(2,1)S(1)}, bf16[1024,8]{0,1:T(8,128)(2,1)}, u32[]{:S(2)}) copy-start(bf16[1024,8]{0,1:T(8,128)(2,1)} %param.10) | copy-start | bytes 49156
  7.2 11.1 %copy-start.5 = (bf16[256,1024]{1,0:T(8,128)(2,1)S(1)}, bf16[256,1024]{1,0:T(8,128)(2,1)}, u32[]{:S(2)}) copy-start(bf16[256,1024]{1,0:T(8,128)(2,1)} %param.17) | copy-start | bytes 1572868
  12.7 27.1 %copy-start.9 = (s32[256]{0:T(256)S(1)}, s32[256]{0:T(256)}, u32[]{:S(2)}) copy-start(s32[256]{0:T(256)} %param.14) | copy-start | bytes 3076
  12.7 23.5 %all-to-all-start.2 = ((bf16[8,80,1024]{2,1,0:T(8,128)(2,1)}), bf16[8,80,1024]{2,1,0:T(8,128)(2,1)S(1)}, u32[]{:S(2)}, u32[]{:S(2)}) async-start(bf16[8,80,1024]{2,1,0:T(8,128)(2,1)} %bitcast.6), calls=%async_computation.2 | async-start | bytes 2621440 | tf_op jit(solution)/shard_map/all_to_all | solution.py:90
  36.2 12.7 %copy-start.1 = (bf16[8,80,1024]{2,1,0:T(8,128)(2,1)}, bf16[8,80,1024]{2,1,0:T(8,128)(2,1)S(1)}, u32[]{:S(2)}) copy-start(bf16[8,80,1024]{2,1,0:T(8,128)(2,1)S(1)} %all-to-all-done.2) | copy-start | bytes 3932164
  36.2 21.7 %all-to-all-start.1 = ((bf16[8,80,1024]{2,1,0:T(8,128)(2,1)}), bf16[8,80,1024]{2,1,0:T(8,128)(2,1)S(1)}, u32[]{:S(2)}, u32[]{:S(2)}) async-start(bf16[8,80,1024]{2,1,0:T(8,128)(2,1)} %bitcast.3), calls=%async_computation.1 | async-start | bytes 2621440 | tf_op jit(solution)/shard_map/all_to_all | solution.py:91
  57.9 8.8 %copy-start.3 = (bf16[8,80,1024]{2,1,0:T(8,128)(2,1)}, bf16[8,80,1024]{2,1,0:T(8,128)(2,1)S(1)}, u32[]{:S(2)}) copy-start(bf16[8,80,1024]{2,1,0:T(8,128)(2,1)S(1)} %all-to-all-done.1) | copy-start | bytes 3932164
  57.9 13.0 %copy-start.4 = (pred[512,640]{1,0:T(8,128)(4,1)S(1)}, pred[512,640]{1,0:T(8,128)(4,1)}, u32[]{:S(2)}) copy-start(pred[512,640]{1,0:T(8,128)(4,1)} %iota_compare_fusion) | copy-start | bytes 983044
  57.9 18.4 %copy-start.7 = (s32[256,2]{0,1:T(2,128)S(1)}, s32[256,2]{0,1:T(2,128)}, u32[]{:S(2)}) copy-start(s32[256,2]{0,1:T(2,128)} %param.13) | copy-start | bytes 6148
  67.4 7.9 %all-to-all-start.4 = ((bf16[8,1,80]{2,1,0:T(2,128)(2,1)}), bf16[8,1,80]{2,1,0:T(2,128)(2,1)S(1)}, u32[]{:S(2)}, u32[]{:S(2)}) async-start(bf16[8,1,80]{2,1,0:T(2,128)(2,1)} %convert_element_type.106), calls=%async_computation.4 | async-start | bytes 8192 | tf_op jit(solution)/shard_map/all_to_all | solution.py:110
  70.7 171.9 %reduce-scatter.3.cloned.1.call-start = ((), (), s32[]{:S(2)}) async-start(), calls=%async_computation.7 | async-start | bytes 10485760 | tf_op jit(solution)/shard_map/reduce_scatter | solution.py:103
  84.3 6.5 %copy-start.2 = (bf16[8,80,1024]{2,1,0:T(8,128)(2,1)S(1)}, bf16[8,80,1024]{2,1,0:T(8,128)(2,1)}, u32[]{:S(2)}) copy-start(bf16[8,80,1024]{2,1,0:T(8,128)(2,1)} %copy-done.1) | copy-start | bytes 3932164
  96.4 293.7 %reduce-scatter.5.cloned.1.call-start = ((), (), s32[]{:S(2)}) async-start(), calls=%async_computation.8 | async-start | bytes 10485760 | tf_op jit(solution)/shard_map/reduce_scatter | solution.py:104
  162.1 57.3 %all-to-all-start.3 = ((bf16[8,80,1024]{2,1,0:T(8,128)(2,1)}), bf16[8,80,1024]{2,1,0:T(8,128)(2,1)S(1)}, u32[]{:S(2)}, u32[]{:S(2)}) async-start(bf16[8,80,1024]{2,1,0:T(8,128)(2,1)} %bitcast.62), calls=%async_computation.3 | async-start | bytes 2621440 | tf_op jit(solution)/shard_map/all_to_all | solution.py:109
Sparse Core Ops, SparseCore 0:
  96.6 146.0 reduce-scatter.2
  245.0 145.1 reduce-scatter.4
where the time goes:
time: 400 us
  waiting for transfers between devices  196 us (49%)
  blocking collectives  104 us (26%)
  matrix products  43.4 us (11%)
  other arithmetic  19.1 us (5%)
  between operations  18.2 us (5%)
  starting transfers between devices  16.2 us (4%)
    reduce_scatter x1, waiting for transfers between devices, on_device(): lax.psum_scatter(second_grad, 'dp', scatter_dimension=0, tiled=True)  145 us
    psum x1, blocking collectives, on_device(): lax.psum((weight_part, jnp.sum(logit_grad, axis=0)), ('expert', 'dp'))  52.9 us
    psum x1, blocking collectives, on_device(): lax.psum((jnp.sum(probs, axis=0), jnp.sum(0.5 * (1.0 + lax.erf(zscore * i...  43.9 us
    reduce_scatter x1, waiting for transfers between devices, on_device(): lax.psum_scatter(first_grad, 'dp', scatter_dimension=1, tiled=True)  21.5 us
    all_to_all x1, waiting for transfers between devices, on_device(): lax.all_to_all(sent_in, 'expert', split_axis=0, concat_axis=0, tiled=True)  16.3 us
    all_to_all x1, waiting for transfers between devices, on_device(): lax.all_to_all(sent_grad, 'expert', split_axis=0, concat_axis=0, tiled=True)  9.05 us
    dot_general x1, matrix products, expert_local(): jnp.dot(active_low.T, scaled_grad, preferred_element_type=jnp.float32)  8.86 us
    dot_general x1, matrix products, expert_local(): jnp.dot(rows_grad, w_second.T, preferred_element_type=jnp.float32)  8.76 us
  transfers between devices with their start and end apart: 6, of which 5 were waited for; matrix products, arithmetic and copies ran while one was open for 9% of the time, Pallas kernels for 0%

commit v1 on v0

--- a/solution.py
+++ b/solution.py
@@ -1,3 +1,4 @@
+import functools
 import jax
 import jax.numpy as jnp
 from jax import lax
@@ -7,6 +8,38 @@
 aux_weight = 1.0
 inv_root_two = 0.7071067811865476
 inv_root_tau = 0.3989422804014327
+
+
+def point_notes_all(field, ndim_at, patch):
+    frame_out = field.shape
+    field_out = field.reshape(
+        *frame_out[:ndim_at], patch, frame_out[ndim_at] // patch, *frame_out[ndim_at + 1 :]
+    )
+    return jnp.moveaxis(field_out, ndim_at, 0)
+
+
+def part_loads(page, d_out):
+    page = jnp.moveaxis(page, 0, d_out)
+    f_next = page.shape
+    return page.reshape(*f_next[:d_out], f_next[d_out] * f_next[d_out + 1], *f_next[d_out + 2 :])
+
+
+def counts_store(chunk, peer_axis, state, base_x):
+    mixed_arr, then = (lax.axis_size(peer_axis), lax.axis_index(peer_axis))
+    formed = point_notes_all(chunk, state, mixed_arr)
+    pile = [formed[then]]
+    for idx in range(1, mixed_arr):
+        row_out = formed[then ^ idx]
+        pile.append(
+            lax.ppermute(
+                row_out, axis_name=peer_axis, perm=[(no, no ^ idx) for no in range(mixed_arr)]
+            )
+        )
+    formed = jnp.stack(pile, axis=0)[then ^ jnp.arange(mixed_arr)]
+    return part_loads(formed, base_x)
+
+
+manage_the_halves = functools.partial(counts_store, peer_axis="expert", state=0, base_x=0)
 
 
 def gelu_tanh(values):
@@ -87,7 +120,7 @@
         .reshape(experts, capacity)
     )
     recv_in, recv_grad, recv_gate = (
-        lax.all_to_all(sent_in, "expert", split_axis=0, concat_axis=0, tiled=True),
+        manage_the_halves(sent_in),
         lax.all_to_all(sent_grad, "expert", split_axis=0, concat_axis=0, tiled=True),
         lax.all_to_all(sent_gate, "expert", split_axis=0, concat_axis=0, tiled=True),
     )

time: 400 us -> 403 us (level)
  waiting for transfers between devices: 196 us -> 186 us
  local copies, waits for them, and re-layouts: 3.41 us -> 10.8 us
    all_to_all x1 -> x0, waiting for transfers between devices: 16.3 us -> none  [on_device(): lax.all_to_all(sent_in, 'expert', split_axis=0, concat_axis=0, tiled=True)]
    ppermute x0 -> x7, waiting for transfers between devices: none -> 15.5 us  [counts_store(): lax.ppermute(row_out, axis_name=peer_axis, perm=[(no, no ^ idx) for no in...]
    all_to_all x1, waiting for transfers between devices: 9.05 us -> 0.01 us  [on_device(): lax.all_to_all(sent_grad, 'expert', split_axis=0, concat_axis=0, tiled=True)]
    ppermute x0 -> x7, starting transfers between devices: none -> 7.97 us  [counts_store(): lax.ppermute(row_out, axis_name=peer_axis, perm=[(no, no ^ idx) for no in...]
    all_to_all x1 -> x0, starting transfers between devices: 5.33 us -> none  [on_device(): lax.all_to_all(sent_in, 'expert', split_axis=0, concat_axis=0, tiled=True)]
    unnamed x23 -> x25, local copies, waits for them, and re-layouts: 0.94 us -> 5.56 us
  transfers between devices with their start and end apart: 6 -> 12, of which waited for: 5 -> 5; matrix products, arithmetic and copies ran while one was open for 9% -> 11% of each run, Pallas kernels for 0% -> 0%
where the time goes in v1:
time: 403 us; the launch traced here: 402 us
  waiting for transfers between devices  186 us (46%)
  blocking collectives  104 us (26%)
  matrix products  44.8 us (11%)
  starting transfers between devices  19.2 us (5%)
  other arithmetic  19.1 us (5%)
  between operations  18.3 us (5%)
  local copies, waits for them, and re-layouts  10.8 us (3%)
    reduce_scatter x1, waiting for transfers between devices, on_device(): lax.psum_scatter(second_grad, 'dp', scatter_dimension=0, tiled=True)  145 us
    psum x1, blocking collectives, on_device(): lax.psum((weight_part, jnp.sum(logit_grad, axis=0)), ('expert', 'dp'))  52.9 us
    psum x1, blocking collectives, on_device(): lax.psum((jnp.sum(probs, axis=0), jnp.sum(0.5 * (1.0 + lax.erf(zscore * i...  43.9 us
    reduce_scatter x1, waiting for transfers between devices, on_device(): lax.psum_scatter(first_grad, 'dp', scatter_dimension=1, tiled=True)  21.5 us
    ppermute x7, waiting for transfers between devices, counts_store(): lax.ppermute(row_out, axis_name=peer_axis, perm=[(no, no ^ idx) for no in...  15.5 us
    dot_general x1, matrix products, expert_local(): hidden = jnp.dot(rows_in, w_first, preferred_element_type=jnp.float32)  9.44 us
    dot_general x1, matrix products, expert_local(): jnp.dot(active_low.T, scaled_grad, preferred_element_type=jnp.float32)  8.86 us
    dot_general x1, matrix products, expert_local(): jnp.dot(rows_grad, w_second.T, preferred_element_type=jnp.float32)  8.75 us
  transfers between devices with their start and end apart: 12, of which 5 were waited for; matrix products, arithmetic and copies ran while one was open for 11% of the time, Pallas kernels for 0%

profile of v1, /device:TPU:0, one launch (start us, length us, event | category | flops | bytes accessed | tf_op | source)
XLA Modules:
  0.0 401.8 jit_solution(2803547650680044972)
XLA Ops:
  7.2 0.9 copy.39
  8.4 1.1 reduce-window.6
  10.1 0.7 multiply_add_fusion.1
  10.8 0.3 fusion.23
  11.1 0.5 convolution_convert_fusion
  11.6 1.0 dynamic-slice_bitcast_fusion
  12.6 0.6 collective-permute-start
  13.2 2.6 collective-permute-start.1
  15.8 1.8 collective-permute-start.3
  17.6 2.7 convolution_convert_fusion.1
  20.2 3.9 all-to-all-start.1
  24.2 1.0 iota_compare_fusion
  25.2 0.3 fusion.39
  25.5 3.0 collective-permute-start.5
  28.5 0.9 bitcast_dynamic-update-slice_fusion.6
  29.5 0.9 bitcast_dynamic-update-slice_fusion.5
  30.4 0.9 bitcast_dynamic-update-slice_fusion.4
  31.4 0.9 bitcast_dynamic-update-slice_fusion.3
  32.3 0.9 bitcast_dynamic-update-slice_fusion.2
  33.3 13.2 %collective-permute-done.5 = bf16[1,80,1024]{2,1,0:T(8,128)(2,1)S(1)} collective-permute-done((bf16[1,80,1024]{2,1,0:T(8,128)(2,1)}, bf16[1,80,1024]{2,1,0:T(8,128)(2,1)S(1)}, u32[]{:S(2)}, u32[]{:S(2)}) %collective-permute-start.5) | collective-permute-done | bytes 163872 | tf_op jit(solution)/shard_map/ppermute | solution.py:34
  46.4 2.3 collective-permute-done.6
  48.8 1.7 gather_fusion
  50.5 9.4 %multiply_convert_fusion = (bf16[640,2048]{1,0:T(8,128)(2,1)}, f32[640,2048]{1,0:T(8,128)}) fusion(bf16[640,1024]{1,0:T(8,128)(2,1)} %bitcast.94, bf16[1,1024,2048]{2,1,0:T(8,128)(2,1)} %param.15), kind=kOutput, calls=%fused_computation.11 | convolution fusion | flops 2696151040 | bytes 13369344 | tf_op jit(solution)/shard_map/dot_general | solution.py:57
  60.0 8.8 %multiply_reduce_fusion = (bf16[640]{0:T(1024)(128)(2,1)S(1)}, f32[640,2048]{1,0:T(8,128)}) fusion(bf16[640,2048]{1,0:T(8,128)(2,1)} %get-tuple-element.27, bf16[640,1024]{1,0:T(8,128)(2,1)S(1)} %bitcast.91, bf16[1,2048,1024]{2,1,0:T(8,128)(2,1)} %param.16), kind=kOutput, calls=%fused_computation.10 | convolution fusion | flops 2688286208 | bytes 13370624 | tf_op jit(solution)/shard_map/dot_general | solution.py:60
  68.8 0.7 convert_element_type.106
  69.4 3.3 all-to-all-start.3
  73.0 0.4 eq.106
  73.4 3.9 all-to-all-done.3
  77.4 0.9 fusion.16
  78.8 0.3 fusion.22
  79.2 7.1 %all_to_all.26 = bf16[8,1,80]{2,1,0:T(2,128)(2,1)S(1)} all-to-all(bf16[8,1,80]{2,1,0:T(2,128)(2,1)S(1)} %all_to_all.21), channel_id=1, replica_groups=mesh['expert'=8,'dp'=4] {'expert'}, dimensions={0} | all-to-all | bytes 2560 | tf_op jit(solution)/shard_map/all_to_all | solution.py:125
  86.3 6.5 %fusion.6 = bf16[640,2048]{1,0:T(8,128)(2,1)S(1)} fusion(f32[640,2048]{1,0:T(8,128)} %get-tuple-element.28, f32[640,2048]{1,0:T(8,128)} %get-tuple-element.30, f32[640]{0:T(1024)S(1)} %reshape.156), kind=kLoop, calls=%fused_computation.9 | loop fusion | flops 27525120 | bytes 13109760 | tf_op jit(solution)/shard_map/convert_element_type | solution.py:63
  92.8 5.7 %fusion.41 = f32[1024,2048]{1,0:T(8,128)} fusion(bf16[640,1024]{1,0:T(8,128)(2,1)S(1)} %bitcast.95, bf16[640,2048]{1,0:T(8,128)(2,1)S(1)} %fusion.6), kind=kOutput, calls=%fused_computation.93 | convolution fusion | flops 2684354560 | bytes 12320768 | tf_op jit(solution)/shard_map/dot_general | solution.py:65
  98.6 8.9 %fusion.17 = f32[2048,1024]{1,0:T(8,128)} fusion(bf16[640,2048]{1,0:T(8,128)(2,1)} %get-tuple-element.27, bf16[640,1024]{1,0:T(8,128)(2,1)} %bitcast.92, f32[640]{0:T(1024)S(1)} %reshape.156), kind=kOutput, calls=%fused_computation.25 | convolution fusion | flops 2686320640 | bytes 12323328 | tf_op jit(solution)/shard_map/dot_general | solution.py:66
  107.5 43.9 %all-reduce.1 = (f32[8]{0:T(128)S(1)}, f32[8]{0:T(128)S(1)}) all-reduce(f32[8]{0:T(128)S(1)} %get-tuple-element.32, f32[8]{0:T(128)S(1)} %get-tuple-element.15), channel_id=1, replica_groups=mesh['expert'=8,'dp'=4] {'expert','dp'}, use_global_device_ids=true, to_apply=%region_16.17 | all-reduce | flops 16 | bytes 128 | tf_op jit(solution)/shard_map/psum | solution.py:94
  151.3 0.6 reduce_sum.162
  153.2 0.6 multiply_reduce_fusion.3
  154.5 0.6 reduce_sum.157
  156.4 0.6 multiply_reduce_fusion.4
  157.7 6.4 %fusion.13 = bf16[640,1024]{1,0:T(8,128)(2,1)} fusion(bf16[640,2048]{1,0:T(8,128)(2,1)S(1)} %fusion.6, bf16[1,1024,2048]{2,1,0:T(8,128)(2,1)} %param.15), kind=kOutput, calls=%fused_computation.20 | convolution fusion | flops 2685009920 | bytes 8126464 | tf_op jit(solution)/shard_map/dot_general | solution.py:74
  164.1 3.9 all-to-all-start.2
  168.5 52.9 %all-reduce = (f32[1024,8]{0,1:T(8,128)}, f32[8]{0:T(128)}) all-reduce(f32[1024,8]{0,1:T(8,128)S(1)} %convolution_bitcast_fusion, f32[8]{0:T(128)S(1)} %get-tuple-element.13), channel_id=1, replica_groups=mesh['expert'=8,'dp'=4] {'expert','dp'}, use_global_device_ids=true, to_apply=%region_22.23 | all-reduce | flops 8200 | bytes 65600 | tf_op jit(solution)/shard_map/psum | solution.py:166
  221.4 0.6 fusion.40
  222.0 1.1 fusion.21
  223.2 21.5 %reduce-scatter.3.cloned.1.call-done = f32[1024,512]{1,0:T(8,128)} async-done(((f32[1024,2048]{1,0:T(8,128)}), f32[1024,512]{1,0:T(8,128)}) %reduce-scatter.3.cloned.1.call-update) | async-done | bytes 2097168 | tf_op jit(solution)/shard_map/reduce_scatter | solution.py:136
  244.7 2.7 convert_bitcast_fusion.1
  247.4 144.8 %reduce-scatter.5.cloned.1.call-done = f32[512,1024]{1,0:T(8,128)} async-done(((f32[2048,1024]{1,0:T(8,128)}), f32[512,1024]{1,0:T(8,128)}) %reduce-scatter.5.cloned.1.call-update) | async-done | bytes 2097168 | tf_op jit(solution)/shard_map/reduce_scatter | solution.py:137
  392.2 2.7 convert_bitcast_fusion
  (64 shorter events, 2.6 us)
Async XLA Ops:
  7.2 3.9 copy-start
  12.6 12.5 %copy-start.4 = (bf16[1024,8]{0,1:T(8,128)(2,1)S(1)}, bf16[1024,8]{0,1:T(8,128)(2,1)}, u32[]{:S(2)}) copy-start(bf16[1024,8]{0,1:T(8,128)(2,1)} %param.10) | copy-start | bytes 49156
  12.6 12.5 %copy-start.6 = (f32[256,8]{0,1:T(8,128)S(1)}, f32[256,8]{0,1:T(8,128)}, u32[]{:S(2)}) copy-start(f32[256,8]{0,1:T(8,128)} %param.12) | copy-start | bytes 24580
  12.6 12.5 %copy-start.8 = (f32[8]{0:T(128)S(1)}, f32[8]{0:T(128)}, u32[]{:S(2)}) copy-start(f32[8]{0:T(128)} %param.11) | copy-start | bytes 100
  12.6 12.8 %collective-permute-start = (bf16[1,80,1024]{2,1,0:T(8,128)(2,1)}, bf16[1,80,1024]{2,1,0:T(8,128)(2,1)}, u32[]{:S(2)}, u32[]{:S(2)}) collective-permute-start(bf16[1,80,1024]{2,1,0:T(8,128)(2,1)} %get-tuple-element.25), channel_id=1, source_target_pairs={{0,4},{4,0},{8,12},{12,8},{16,20},{20,16},{24,28},{28,24},{1,5},{5... | collective-permute-start | bytes 491528 | tf_op jit(solution)/shard_map/ppermute | solution.py:34
  13.2 16.2 %collective-permute-start.1 = (bf16[1,80,1024]{2,1,0:T(8,128)(2,1)}, bf16[1,80,1024]{2,1,0:T(8,128)(2,1)}, u32[]{:S(2)}, u32[]{:S(2)}) collective-permute-start(bf16[1,80,1024]{2,1,0:T(8,128)(2,1)} %get-tuple-element.24), channel_id=1, source_target_pairs={{0,8},{4,12},{8,0},{12,4},{16,24},{20,28},{24,16},{28,20},{1,9},{5... | collective-permute-start | bytes 491528 | tf_op jit(solution)/shard_map/ppermute | solution.py:34
  15.8 14.7 %collective-permute-start.2 = (bf16[1,80,1024]{2,1,0:T(8,128)(2,1)}, bf16[1,80,1024]{2,1,0:T(8,128)(2,1)}, u32[]{:S(2)}, u32[]{:S(2)}) collective-permute-start(bf16[1,80,1024]{2,1,0:T(8,128)(2,1)} %get-tuple-element.23), channel_id=1, source_target_pairs={{0,12},{4,8},{8,4},{12,0},{16,28},{20,24},{24,20},{28,16},{1,13},{... | collective-permute-start | bytes 491528 | tf_op jit(solution)/shard_map/ppermute | solution.py:34
  15.8 15.6 %collective-permute-start.3 = (bf16[1,80,1024]{2,1,0:T(8,128)(2,1)}, bf16[1,80,1024]{2,1,0:T(8,128)(2,1)}, u32[]{:S(2)}, u32[]{:S(2)}) collective-permute-start(bf16[1,80,1024]{2,1,0:T(8,128)(2,1)} %get-tuple-element.22), channel_id=1, source_target_pairs={{0,16},{4,20},{8,24},{12,28},{16,0},{20,4},{24,8},{28,12},{1,17},{... | collective-permute-start | bytes 491528 | tf_op jit(solution)/shard_map/ppermute | solution.py:34
  17.6 7.9 %copy-start.7 = (s32[256]{0:T(256)S(1)}, s32[256]{0:T(256)}, u32[]{:S(2)}) copy-start(s32[256]{0:T(256)} %param.14) | copy-start | bytes 3076
  17.6 14.7 %collective-permute-start.4 = (bf16[1,80,1024]{2,1,0:T(8,128)(2,1)}, bf16[1,80,1024]{2,1,0:T(8,128)(2,1)}, u32[]{:S(2)}, u32[]{:S(2)}) collective-permute-start(bf16[1,80,1024]{2,1,0:T(8,128)(2,1)} %get-tuple-element.21), channel_id=1, source_target_pairs={{0,20},{4,16},{8,28},{12,24},{16,4},{20,0},{24,12},{28,8},{1,21},{... | collective-permute-start | bytes 491528 | tf_op jit(solution)/shard_map/ppermute | solution.py:34
  20.2 39.8 %all-to-all-start.1 = ((bf16[8,80,1024]{2,1,0:T(8,128)(2,1)}), bf16[8,80,1024]{2,1,0:T(8,128)(2,1)S(1)}, u32[]{:S(2)}, u32[]{:S(2)}) async-start(bf16[8,80,1024]{2,1,0:T(8,128)(2,1)} %bitcast.3), calls=%async_computation.1 | async-start | bytes 2621440 | tf_op jit(solution)/shard_map/all_to_all | solution.py:124
  25.5 20.9 %collective-permute-start.5 = (bf16[1,80,1024]{2,1,0:T(8,128)(2,1)}, bf16[1,80,1024]{2,1,0:T(8,128)(2,1)S(1)}, u32[]{:S(2)}, u32[]{:S(2)}) collective-permute-start(bf16[1,80,1024]{2,1,0:T(8,128)(2,1)} %get-tuple-element.20), channel_id=1, source_target_pairs={{0,24},{4,28},{8,16},{12,20},{16,8},{20,12},{24,0},{28,4},{1,25},{... | collective-permute-start | bytes 491528 | tf_op jit(solution)/shard_map/ppermute | solution.py:34
  29.4 19.4 %collective-permute-start.6 = (bf16[1,80,1024]{2,1,0:T(8,128)(2,1)}, bf16[1,80,1024]{2,1,0:T(8,128)(2,1)S(1)}, u32[]{:S(2)}, u32[]{:S(2)}) collective-permute-start(bf16[1,80,1024]{2,1,0:T(8,128)(2,1)} %get-tuple-element.19), channel_id=1, source_target_pairs={{0,28},{4,24},{8,20},{12,16},{16,12},{20,8},{24,4},{28,0},{1,29},{... | collective-permute-start | bytes 491528 | tf_op jit(solution)/shard_map/ppermute | solution.py:34
  60.0 8.8 %copy-start.1 = (bf16[8,80,1024]{2,1,0:T(8,128)(2,1)}, bf16[8,80,1024]{2,1,0:T(8,128)(2,1)S(1)}, u32[]{:S(2)}) copy-start(bf16[8,80,1024]{2,1,0:T(8,128)(2,1)S(1)} %all-to-all-done.1) | copy-start | bytes 3932164
  60.0 13.0 %copy-start.3 = (pred[512,640]{1,0:T(8,128)(4,1)S(1)}, pred[512,640]{1,0:T(8,128)(4,1)}, u32[]{:S(2)}) copy-start(pred[512,640]{1,0:T(8,128)(4,1)} %iota_compare_fusion) | copy-start | bytes 983044
  60.0 18.4 %copy-start.5 = (s32[256,2]{0,1:T(2,128)S(1)}, s32[256,2]{0,1:T(2,128)}, u32[]{:S(2)}) copy-start(s32[256,2]{0,1:T(2,128)} %param.13) | copy-start | bytes 6148
  69.4 7.9 %all-to-all-start.3 = ((bf16[8,1,80]{2,1,0:T(2,128)(2,1)}), bf16[8,1,80]{2,1,0:T(2,128)(2,1)S(1)}, u32[]{:S(2)}, u32[]{:S(2)}) async-start(bf16[8,1,80]{2,1,0:T(2,128)(2,1)} %convert_element_type.106), calls=%async_computation.3 | async-start | bytes 8192 | tf_op jit(solution)/shard_map/all_to_all | solution.py:143
  72.8 171.9 %reduce-scatter.3.cloned.1.call-start = ((), (), s32[]{:S(2)}) async-start(), calls=%async_computation.6 | async-start | bytes 10485760 | tf_op jit(solution)/shard_map/reduce_scatter | solution.py:136
  86.3 6.5 %copy-start.2 = (bf16[8,80,1024]{2,1,0:T(8,128)(2,1)S(1)}, bf16[8,80,1024]{2,1,0:T(8,128)(2,1)}, u32[]{:S(2)}) copy-start(bf16[8,80,1024]{2,1,0:T(8,128)(2,1)} %gather_fusion) | copy-start | bytes 3932164
  98.5 293.7 %reduce-scatter.5.cloned.1.call-start = ((), (), s32[]{:S(2)}) async-start(), calls=%async_computation.7 | async-start | bytes 10485760 | tf_op jit(solution)/shard_map/reduce_scatter | solution.py:137
  164.1 57.3 %all-to-all-start.2 = ((bf16[8,80,1024]{2,1,0:T(8,128)(2,1)}), bf16[8,80,1024]{2,1,0:T(8,128)(2,1)S(1)}, u32[]{:S(2)}, u32[]{:S(2)}) async-start(bf16[8,80,1024]{2,1,0:T(8,128)(2,1)} %bitcast.93), calls=%async_computation.2 | async-start | bytes 2621440 | tf_op jit(solution)/shard_map/all_to_all | solution.py:142
Sparse Core Ops, SparseCore 0:
  98.6 145.9 reduce-scatter.2
  247.0 145.1 reduce-scatter.4
